TPU v7x, 32 devices: a whole 2x2x4 slice. The times are simulated.
32 devices in a mesh: frame: 4 (over x, core), seq: 8 (over z, y).
Axes of the slice: x: 2, y: 2, z: 4, core: 2. Of those that a mesh axis runs over, the one named last changes fastest.
Arguments:
- vit_states: bfloat16 [64, 256, 1280], P(('frame', 'seq')), may hold values from -6 to 6
- frame_slot: int32 [32], replicated, may hold values from 0 to 63, as said below
- patch_count: int32 [32], replicated, may hold values from 208 to 256, as said below
- vis_start: int32 [32], replicated, may hold values from 0 to 4095, as said below
- text_embed: bfloat16 [128, 32, 4096], P(None, ('frame', 'seq')), may hold values from -6 to 6
- vit_ln_gain: float32 [1280], replicated, may hold values from 0.25 to 1.75
- vit_ln_bias: float32 [1280], replicated, may hold values from -1.5 to 1.5
- vit_qkv_w: bfloat16 [1280, 3840], P('seq'), may hold values from -0.15625 to 0.15625
- vit_qkv_b: float32 [3840], replicated, may hold values from -1.5 to 1.5
- vit_out_w: bfloat16 [1280, 1280], P('seq'), may hold values from -0.15625 to 0.15625
- vit_out_b: float32 [1280], replicated, may hold values from -1.5 to 1.5
- proj_w: bfloat16 [1280, 4096], replicated, may hold values from -0.15625 to 0.15625
- proj_b: float32 [4096], replicated, may hold values from -1.5 to 1.5
- attn_gain: float32 [4096], replicated, may hold values from 0.25 to 1.75
- wq: bfloat16 [4096, 2048], P(None, 'frame'), may hold values from -0.09375 to 0.09375
- wk: bfloat16 [4096, 1024], P(None, 'frame'), may hold values from -0.09375 to 0.09375
- wv: bfloat16 [4096, 1024], P(None, 'frame'), may hold values from -0.09375 to 0.09375
- wo: bfloat16 [2048, 4096], P('frame'), may hold values from -0.125 to 0.125
Outputs:
- mixed: bfloat16 [128, 32, 4096], P(None, ('frame', 'seq'))
Inputs may be any that keep to these rules, and one draw needn't show every extreme that they name: Frame t sits in slot frame_slot[t]; slot k of the device with index d (axes frame then seq) is d * 2 + k; no slot holds two frames. The two devices with frame indices 2i and 2i+1 and the same seq index hold exactly two frames between them; some device holds 2 frames. `patch_count`: A multiple of 4; some frame has 256 patches. Frame t's patch_count[t] / 4 visual positions start at vis_start[t] and lie within positions t * 128 to (t + 1) * 128 - 1.
All inputs are finite; a program needn't handle non-finite values.
Results may differ from a plain program's by a relative error of at most 0.015.
Values may be sent and summed in bfloat16 or wider, within the bound.
A program may use at most 128 MiB of HBM per device.

v0:
```python
import math
import jax
import jax.numpy as jnp
from jax import lax
from jax.sharding import PartitionSpec as P

VHEADS = 16
HEAD_WIDTH = 128
rope_theta = 500000.0
vit_epsilon = 1e-06
norm_epsilon = 1e-05
masked_score = -1e30


def partner_2(value, axis, stride):
    mask = 2**stride
    pairs = [(source, source ^ mask) for source in range(lax.axis_size(axis))]
    return lax.ppermute(value, axis, pairs)


def apply_rotary(values, rotary_angles):
    half_width = values.shape[-1] // 2
    first_half = values[..., :half_width]
    second_half = values[..., half_width:]
    cosine = jnp.cos(rotary_angles)
    sine_part = jnp.sin(rotary_angles)
    return jnp.concatenate(
        [
            first_half * cosine - second_half * sine_part,
            second_half * cosine + first_half * sine_part,
        ],
        axis=-1,
    )


def rope_angles(positions, head_size):
    exponents = jnp.arange(0, head_size, 2).astype(jnp.float32) / head_size
    inverse = jnp.power(jnp.float32(rope_theta), -exponents)
    return positions.astype(jnp.float32)[:, None] * inverse[None, :]


def add_columns(left, shard_piece):
    return jnp.dot(left, shard_piece, preferred_element_type=jnp.float32)


def per_device(
    vit_states,
    frame_slot,
    patch_count,
    vis_start,
    text_embed,
    vit_ln_gain,
    vit_ln_bias,
    vit_qkv_w,
    vit_qkv_b,
    vit_out_w,
    vit_out_b,
    proj_w,
    proj_b,
    attn_gain,
    wq,
    wk,
    wv,
    wo,
):
    frames_n = lax.axis_size("frame")
    seqs_n = lax.axis_size("seq")
    devices_n = frames_n * seqs_n
    my_frame = lax.axis_index("frame")
    my_seq = lax.axis_index("seq")
    my_device = my_frame * seqs_n + my_seq
    slots_held = vit_states.shape[0]
    frame_max = vit_states.shape[1]
    width_vit = vit_states.shape[2]
    vis_max = frame_max // 4
    own_rows = text_embed.shape[0]
    laps = (vis_max + devices_n - 1) // devices_n
    frame_ids = jnp.arange(frame_slot.shape[0])
    holder = frame_slot // slots_held
    holder_frame = holder // seqs_n
    pair_low = (holder_frame - holder_frame % 2) * seqs_n + holder % seqs_n
    pair_order = holder_frame % 2 * slots_held + frame_slot % slots_held
    same_pair = pair_low[:, None] == pair_low[None, :]
    earlier = pair_order[None, :] < pair_order[:, None]
    pair_rank = jnp.sum((same_pair & earlier).astype(jnp.int32), axis=1)
    partner = partner_2(vit_states, "frame", 0)
    low_side = my_frame % 2 == 0
    four_slots = jnp.where(
        low_side,
        jnp.concatenate([vit_states, partner], 0),
        jnp.concatenate([partner, vit_states], 0),
    )
    my_low = (my_frame - my_frame % 2) * seqs_n + my_seq
    picked = (pair_low == my_low) & (pair_rank == my_frame % 2)
    my_frame_id = jnp.sum(jnp.where(picked, frame_ids, 0))
    my_order = jnp.sum(jnp.where(picked, pair_order, 0))
    states = lax.dynamic_slice_in_dim(four_slots, my_order, 1, 0)
    slots_n = 1
    slot_frames = jnp.reshape(my_frame_id, (1,))
    slot_live = jnp.ones((1,), jnp.bool_)
    source_device = pair_low + pair_rank * seqs_n
    slot_count = jnp.where(slot_live, patch_count[slot_frames], frame_max)
    slot_start = vis_start[slot_frames]
    patch_rows = states.reshape(slots_n * frame_max, width_vit)
    rows_wide = patch_rows.astype(jnp.float32)
    average = jnp.mean(rows_wide, axis=1, keepdims=True)
    centred = rows_wide - average
    spread = jnp.mean(centred * centred, axis=1, keepdims=True)
    normed_states = (centred * lax.rsqrt(spread + vit_epsilon) * vit_ln_gain + vit_ln_bias).astype(
        jnp.bfloat16
    )
    projected_vit = add_columns(normed_states, lax.all_gather(vit_qkv_w, "seq", axis=0, tiled=True))
    projected_vit = (projected_vit + vit_qkv_b).astype(jnp.bfloat16)
    head_size = width_vit // VHEADS
    shaped = projected_vit.reshape(slots_n, frame_max, 3, VHEADS, head_size)
    scores = jnp.einsum(
        "sqhd,skhd->shqk", shaped[:, :, 0], shaped[:, :, 1], preferred_element_type=jnp.float32
    ) / math.sqrt(head_size)
    key_live = jnp.arange(frame_max)[None, :] < slot_count[:, None]
    scores = jnp.where(key_live[:, None, None, :], scores, masked_score)
    highest = jnp.max(scores, axis=-1, keepdims=True)
    weights = jnp.exp(scores - highest)
    probabilities = (weights / jnp.sum(weights, axis=-1, keepdims=True)).astype(jnp.bfloat16)
    context_vit = jnp.einsum(
        "shqk,skhd->sqhd", probabilities, shaped[:, :, 2], preferred_element_type=jnp.float32
    ).astype(jnp.bfloat16)
    context_vit = context_vit.reshape(patch_rows.shape[0], width_vit)
    attended = add_columns(context_vit, lax.all_gather(vit_out_w, "seq", axis=0, tiled=True))
    hidden = (rows_wide + attended + vit_out_b).astype(jnp.bfloat16)
    pooled = jnp.mean(
        hidden.astype(jnp.float32).reshape(slots_n, vis_max, 4, width_vit), axis=2
    ).astype(jnp.bfloat16)
    owners = jnp.arange(devices_n)
    lap_ids = jnp.arange(laps)
    distance = jnp.mod(owners[:, None] - slot_start[None, :], devices_n)
    token_ids = distance[:, :, None] + lap_ids[None, None, :] * devices_n
    sent_live = (token_ids < (slot_count // 4)[None, :, None]) & slot_live[None, :, None]
    token_clip = jnp.minimum(token_ids, vis_max - 1)
    slot_ids = jnp.arange(slots_n)[None, :, None]
    outgoing = jnp.where(
        sent_live[..., None], pooled[slot_ids, token_clip], jnp.zeros((), jnp.bfloat16)
    )
    arrived = lax.all_to_all(outgoing, ("frame", "seq"), split_axis=0, concat_axis=0, tiled=True)
    local_ids = jnp.arange(own_rows)
    positions = local_ids * devices_n + my_device
    token_frame = positions // own_rows
    within = positions - vis_start[token_frame]
    is_visual = (within >= 0) & (within < patch_count[token_frame] // 4)
    within_clip = jnp.clip(within, 0, vis_max - 1)
    flat_index = source_device[token_frame] * slots_n * laps + within_clip // devices_n
    table = arrived.reshape(devices_n * slots_n * laps, arrived.shape[-1])
    fetched = table[flat_index]
    fetched = (jnp.dot(fetched, proj_w, preferred_element_type=jnp.float32) + proj_b).astype(
        jnp.bfloat16
    )
    text_rows = text_embed.reshape(own_rows, text_embed.shape[-1])
    merged = jnp.where(is_visual[:, None], fetched, text_rows)
    merged_wide = merged.astype(jnp.float32)
    normed_tok = (
        merged_wide
        * lax.rsqrt(jnp.mean(merged_wide * merged_wide, axis=1, keepdims=True) + norm_epsilon)
        * attn_gain
    ).astype(jnp.bfloat16)
    shard_piece = lax.all_gather(normed_tok, "frame", axis=0, tiled=True)
    projected = jnp.concatenate(
        [
            jnp.dot(shard_piece, wq, preferred_element_type=jnp.float32),
            jnp.dot(shard_piece, wk, preferred_element_type=jnp.float32),
            jnp.dot(shard_piece, wv, preferred_element_type=jnp.float32),
        ],
        axis=1,
    )
    query_width = wq.shape[1]
    kv_width = wk.shape[1]
    group_rows = projected.shape[0]
    kv_heads = kv_width // HEAD_WIDTH
    query_heads = query_width // HEAD_WIDTH
    row_ids = jnp.arange(group_rows)
    group_positions = row_ids % own_rows * devices_n + row_ids // own_rows * seqs_n + my_seq
    rotary_angles = rope_angles(group_positions, HEAD_WIDTH)[:, None, :]
    query_matrix = apply_rotary(
        projected[:, :query_width].reshape(group_rows, query_heads, HEAD_WIDTH), rotary_angles
    ).astype(jnp.bfloat16)
    keys_own = apply_rotary(
        projected[:, query_width : query_width + kv_width].reshape(
            group_rows, kv_heads, HEAD_WIDTH
        ),
        rotary_angles,
    ).astype(jnp.bfloat16)
    values_own = (
        projected[:, query_width + kv_width :]
        .astype(jnp.bfloat16)
        .reshape(group_rows, kv_heads, HEAD_WIDTH)
    )
    grouped_rows = query_matrix.reshape(group_rows, kv_heads, query_heads // kv_heads, HEAD_WIDTH)
    group_size = query_heads // kv_heads
    start_state = (
        jnp.full((kv_heads, group_size, group_rows), masked_score, jnp.float32),
        jnp.zeros((kv_heads, group_size, group_rows), jnp.float32),
        jnp.zeros((kv_heads, group_size, group_rows, HEAD_WIDTH), jnp.float32),
    )
    carry = start_state
    key_piece = lax.all_gather(keys_own, "seq", axis=0, tiled=True)
    value_piece = lax.all_gather(values_own, "seq", axis=0, tiled=True)
    piece_rows = key_piece.shape[0]
    inner_rows = math.gcd(piece_rows, 1024)
    steps_n = piece_rows // inner_rows
    key_blocks = key_piece.reshape(steps_n, inner_rows, kv_heads, HEAD_WIDTH)
    value_blocks = value_piece.reshape(steps_n, inner_rows, kv_heads, HEAD_WIDTH)
    block_offsets = inner_rows * jnp.arange(steps_n)

    def visit(running, operands):
        running_max, denominator, weighted = running
        key_block, value_block, block_offset = operands
        gathered_ids = block_offset + jnp.arange(inner_rows)
        seq_of = gathered_ids // group_rows
        inner_ids = gathered_ids % group_rows
        key_positions = inner_ids % own_rows * devices_n + inner_ids // own_rows * seqs_n + seq_of
        block_scores = jnp.einsum(
            "qkgd,nkd->kgqn", grouped_rows, key_block, preferred_element_type=jnp.float32
        ) / math.sqrt(HEAD_WIDTH)
        allowed = key_positions[None, :] <= group_positions[:, None]
        block_scores = jnp.where(allowed[None, None], block_scores, masked_score)
        new_max = jnp.maximum(running_max, jnp.max(block_scores, axis=-1))
        expd = jnp.where(allowed[None, None], jnp.exp(block_scores - new_max[..., None]), 0.0)
        rescale = jnp.exp(running_max - new_max)
        denominator = denominator * rescale + jnp.sum(expd, axis=-1)
        weighted = weighted * rescale[..., None] + jnp.einsum(
            "kgqn,nkd->kgqd",
            expd.astype(jnp.bfloat16),
            value_block,
            preferred_element_type=jnp.float32,
        )
        return ((new_max, denominator, weighted), None)

    carry, unused = lax.scan(visit, carry, (key_blocks, value_blocks, block_offsets))
    final_max, denominator, weighted = carry
    context_tok = (weighted / denominator[..., None]).astype(jnp.bfloat16)
    context_tok = jnp.transpose(context_tok, (2, 0, 1, 3)).reshape(group_rows, query_width)
    summed = lax.psum_scatter(
        jnp.dot(context_tok, wo, preferred_element_type=jnp.float32).astype(jnp.bfloat16),
        "frame",
        scatter_dimension=0,
        tiled=True,
    )
    return summed.reshape(own_rows, 1, wo.shape[1])


def solution(mesh):
    return jax.shard_map(
        per_device,
        mesh=mesh,
        in_specs=(
            P(("frame", "seq"), None, None),
            P(),
            P(),
            P(),
            P(None, ("frame", "seq"), None),
            P(),
            P(),
            P("seq", None),
            P(),
            P("seq", None),
            P(),
            P(),
            P(),
            P(),
            P(None, "frame"),
            P(None, "frame"),
            P(None, "frame"),
            P("frame", None),
        ),
        out_specs=P(None, ("frame", "seq"), None),
        check_vma=False,
    )
```

profile of v0, /device:TPU:0, one launch (start us, length us, event | category | flops | bytes accessed | tf_op | source)
XLA Modules:
  0.0 512.4 jit_solution(6202785359800764585)
XLA Ops:
  26.0 1.9 convert_reduce_fusion
  28.2 126.3 %all-gather.6.cloned.1.call-done = bf16[1280,3840]{1,0:T(8,128)(2,1)} async-done(((bf16[160,3840]{1,0:T(8,128)(2,1)}), bf16[1280,3840]{1,0:T(8,128)(2,1)}) %all-gather.6.cloned.1.call-update) | async-done | bytes 9830416 | tf_op jit(solution)/shard_map/all_gather | solution.py:112
  154.5 7.9 %fusion.48 = bf16[256,3840]{1,0:T(8,128)(2,1)} fusion(bf16[1280,3840]{1,0:T(8,128)(2,1)} %all-gather.6.cloned.1.call-done, f32[3840]{0:T(1024)S(1)} %copy-done.5, bf16[1,256,1280]{2,1,0:T(8,128)(2,1)S(1)} %get-tuple-element.277, f32[1280]{0:T(1024)S(1)} %copy-done.6, f32[1280]{0:T(1024)S(1)} %copy-done.7, f32[256]{0:T(256)S(1)} %add_rsqrt_fusion, ...), kind=kOutput, calls=%fused_computation.75 | convolution fusion | flops 2520514560 | bytes 12479488 | tf_op jit(solution)/shard_map/dot_general | solution.py:43
  162.4 4.0 copy.73
  166.4 2.0 fusion.72
  168.5 1.7 fusion.102
  171.8 44.6 %all-gather.8.cloned.1.call-done = bf16[1280,1280]{1,0:T(8,128)(2,1)} async-done(((bf16[160,1280]{1,0:T(8,128)(2,1)}), bf16[1280,1280]{1,0:T(8,128)(2,1)}) %all-gather.8.cloned.1.call-update) | async-done | bytes 3276816 | tf_op jit(solution)/shard_map/all_gather | solution.py:128
  216.4 4.0 fusion.55
  226.7 3.3 all-to-all-start
  230.3 7.7 %all-to-all-done = bf16[32,1,2,1280]{3,2,1,0:T(2,128)(2,1)S(1)} async-done(((bf16[32,1,2,1280]{3,2,1,0:T(2,128)(2,1)}), bf16[32,1,2,1280]{3,2,1,0:T(2,128)(2,1)S(1)}, u32[]{:S(2)}, u32[]{:S(2)}) %all-to-all-start) | async-done | bytes 163872 | tf_op jit(solution)/shard_map/all_to_all | solution.py:143
  239.0 6.3 %multiply_reduce_fusion = (f32[128]{0:T(128)S(1)}, f32[128,4096]{1,0:T(8,128)S(1)}) fusion(bf16[128,1,4096]{2,0,1:T(8,128)(2,1)} %param.24, f32[4096]{0:T(1024)S(1)} %copy-done.3, bf16[128,1280]{1,0:T(8,128)(2,1)S(1)} %gather_fusion.4, bf16[1280,4096]{1,0:T(8,128)(2,1)} %param.31, pred[128]{0:T(512)(128)(4,1)S(1)} %compare_and_fusion.1), kind=kOutput, calls=%fused_computation.93 | convolution fusion | flops 1345322880 | bytes 13976192 | tf_op jit(solution)/shard_map/dot_general | solution.py:153
  247.5 32.0 %all-gather.10.cloned.1.call-done = bf16[512,4096]{1,0:T(8,128)(2,1)} async-done(((bf16[128,4096]{1,0:T(8,128)(2,1)}), bf16[512,4096]{1,0:T(8,128)(2,1)}) %all-gather.10.cloned.1.call-update) | async-done | bytes 4194320 | tf_op jit(solution)/shard_map/all_gather | solution.py:164
  279.5 3.5 fusion.103
  284.5 4.2 convolution_convert_fusion.1
  289.6 6.0 %fusion.104 = f32[512,512]{0,1:T(8,128)S(1)} fusion(bf16[512,4096]{1,0:T(8,128)(2,1)} %all-gather.10.cloned.1.call-done, bf16[4096,512]{1,0:T(8,128)(2,1)} %param.34), kind=kOutput, calls=%fused_computation.213 | convolution fusion | flops 2147483648 | bytes 9437184 | tf_op jit(solution)/shard_map/dot_general | solution.py:167
  296.7 37.0 %all-gather.12.cloned.1.call-done = bf16[4096,2,128]{2,0,1:T(8,128)(2,1)} async-done(((bf16[512,2,128]{2,0,1:T(8,128)(2,1)}), bf16[4096,2,128]{2,0,1:T(8,128)(2,1)}) %all-gather.12.cloned.1.call-update) | async-done | bytes 2097168 | tf_op jit(solution)/shard_map/all_gather | solution.py:203
  333.7 49.7 %all-gather.14.cloned.1.call-done = bf16[4096,2,128]{2,0,1:T(8,128)(2,1)} async-done(((bf16[512,2,128]{2,0,1:T(8,128)(2,1)}), bf16[4096,2,128]{2,0,1:T(8,128)(2,1)}) %all-gather.14.cloned.1.call-update) | async-done | bytes 2097168 | tf_op jit(solution)/shard_map/all_gather | solution.py:204
  383.3 71.8 %while.20 = (s32[]{:T(128)}, f32[2,2,512]{2,1,0:T(2,128)S(1)}, f32[2,2,512]{2,1,0:T(2,128)S(1)}, f32[2,2,512,128]{3,2,1,0:T(8,128)S(1)}, s32[4]{0:T(128)S(1)}, /...) while((s32[]{:T(128)}, f32[2,2,512]{2,1,0:T(2,128)S(1)}, ...), condition=%wide.region_12.13_spmd.clone, body=%wide.region_9.12_spmd.clone.sunk | while | flops 1102377984 | bytes 64631976 | solution.py:236
  385.0 5.9 %fusion.134 = (f32[2,2,512]{2,1,0:T(2,128)S(1)}, f32[2,1024,512,2]{2,1,3,0:T(8,128)}) fusion(pred[512,1024]{0,1:T(8,128)(4,1)S(1)} %broadcast_compare_fusion.2, bf16[512,2,2,128]{3,0,2,1:T(8,128)(2,1)S(1)} %get-tuple-element.390, bf16[4,1024,2,128]{3,1,0,2:T(8,128)(2,1)} %get-tuple-element.389, s32[]{:T(128)} %get-tuple-element.373), kind=kOutput, calls=%fused_computation.8.clone.1 | convolution fusion | flops 543160320 | bytes 9970176 | tf_op jit(solution)/shard_map/while/body/eval_jaxpr/qkgd,nkd->kgqn/dot_general | solution.py:219
  390.8 4.6 fusion.136
  396.7 4.6 fusion.138
  402.9 5.9 %fusion.134 = (f32[2,2,512]{2,1,0:T(2,128)S(1)}, f32[2,1024,512,2]{2,1,3,0:T(8,128)}) fusion(pred[512,1024]{0,1:T(8,128)(4,1)S(1)} %broadcast_compare_fusion.2, bf16[512,2,2,128]{3,0,2,1:T(8,128)(2,1)S(1)} %get-tuple-element.390, bf16[4,1024,2,128]{3,1,0,2:T(8,128)(2,1)} %get-tuple-element.389, s32[]{:T(128)} %get-tuple-element.373), kind=kOutput, calls=%fused_computation.8.clone.1 | convolution fusion | flops 543160320 | bytes 9970176 | tf_op jit(solution)/shard_map/while/body/eval_jaxpr/qkgd,nkd->kgqn/dot_general | solution.py:219
  408.8 4.6 fusion.136
  414.6 4.6 fusion.138
  420.9 5.9 %fusion.134 = (f32[2,2,512]{2,1,0:T(2,128)S(1)}, f32[2,1024,512,2]{2,1,3,0:T(8,128)}) fusion(pred[512,1024]{0,1:T(8,128)(4,1)S(1)} %broadcast_compare_fusion.2, bf16[512,2,2,128]{3,0,2,1:T(8,128)(2,1)S(1)} %get-tuple-element.390, bf16[4,1024,2,128]{3,1,0,2:T(8,128)(2,1)} %get-tuple-element.389, s32[]{:T(128)} %get-tuple-element.373), kind=kOutput, calls=%fused_computation.8.clone.1 | convolution fusion | flops 543160320 | bytes 9970176 | tf_op jit(solution)/shard_map/while/body/eval_jaxpr/qkgd,nkd->kgqn/dot_general | solution.py:219
  426.7 4.6 fusion.136
  432.6 4.6 fusion.138
  438.8 5.9 %fusion.134 = (f32[2,2,512]{2,1,0:T(2,128)S(1)}, f32[2,1024,512,2]{2,1,3,0:T(8,128)}) fusion(pred[512,1024]{0,1:T(8,128)(4,1)S(1)} %broadcast_compare_fusion.2, bf16[512,2,2,128]{3,0,2,1:T(8,128)(2,1)S(1)} %get-tuple-element.390, bf16[4,1024,2,128]{3,1,0,2:T(8,128)(2,1)} %get-tuple-element.389, s32[]{:T(128)} %get-tuple-element.373), kind=kOutput, calls=%fused_computation.8.clone.1 | convolution fusion | flops 543160320 | bytes 9970176 | tf_op jit(solution)/shard_map/while/body/eval_jaxpr/qkgd,nkd->kgqn/dot_general | solution.py:219
  444.7 4.6 fusion.136
  450.5 4.6 fusion.138
  455.6 6.6 %convolution_convert_fusion = bf16[512,4096]{1,0:T(8,128)(2,1)} fusion(bf16[512,512]{0,1:T(8,128)(2,1)S(1)} %bitcast.138, bf16[512,4096]{1,0:T(8,128)(2,1)} %param.37), kind=kOutput, calls=%fused_computation.73 | convolution fusion | flops 2149580800 | bytes 8912896 | tf_op jit(solution)/shard_map/dot_general | solution.py:241
  462.3 43.3 %reduce-scatter.2.cloned.1.call-done = bf16[128,4096]{1,0:T(8,128)(2,1)} async-done(((bf16[512,4096]{1,0:T(8,128)(2,1)}), bf16[128,4096]{1,0:T(8,128)(2,1)}) %reduce-scatter.2.cloned.1.call-update) | async-done | bytes 1048592 | tf_op jit(solution)/shard_map/reduce_scatter | solution.py:240
  (127 shorter events, 39.2 us)
Async XLA Ops:
  6.5 272.9 %copy-start = (bf16[4096,256]{1,0:T(8,128)(2,1)S(1)}, bf16[4096,256]{1,0:T(8,128)(2,1)}, u32[]{:S(2)}) copy-start(bf16[4096,256]{1,0:T(8,128)(2,1)} %param.35) | copy-start | bytes 6291460
  6.5 148.0 %copy-start.7 = (f32[1280]{0:T(1024)S(1)}, f32[1280]{0:T(1024)}, u32[]{:S(2)}) copy-start(f32[1280]{0:T(1024)} %param.25) | copy-start | bytes 15364
  6.5 148.0 %copy-start.6 = (f32[1280]{0:T(1024)S(1)}, f32[1280]{0:T(1024)}, u32[]{:S(2)}) copy-start(f32[1280]{0:T(1024)} %param.26) | copy-start | bytes 15364
  6.5 148.0 %copy-start.5 = (f32[3840]{0:T(1024)S(1)}, f32[3840]{0:T(1024)}, u32[]{:S(2)}) copy-start(f32[3840]{0:T(1024)} %param.28) | copy-start | bytes 46084
  6.5 148.0 %all-gather.6.cloned.1.call-start = ((), (), s32[]{:S(2)}) async-start(), calls=%async_computation.2 | async-start | bytes 11059200 | tf_op jit(solution)/shard_map/all_gather | solution.py:112
  7.3 209.1 %all-gather.8.cloned.1.call-start = ((), (), s32[]{:S(2)}) async-start(), calls=%async_computation.3 | async-start | bytes 3686400 | tf_op jit(solution)/shard_map/all_gather | solution.py:128
  7.3 18.7 %collective-permute-start = (bf16[2,256,1280]{2,1,0:T(8,128)(2,1)}, bf16[2,256,1280]{2,1,0:T(8,128)(2,1)}, u32[]{:S(2)}, u32[]{:S(2)}) collective-permute-start(bf16[2,256,1280]{2,1,0:T(8,128)(2,1)} %param.20), channel_id=1, source_target_pairs={{0,8},{8,0},{16,24},{24,16},{1,9},{9,1},{17,25},{25,17},{2,10},{10... | collective-permute-start | bytes 3932168 | tf_op jit(solution)/shard_map/ppermute | solution.py:18
  170.2 46.2 %copy-start.8 = (f32[1280]{0:T(1024)S(1)}, f32[1280]{0:T(1024)}, u32[]{:S(2)}) copy-start(f32[1280]{0:T(1024)} %param.30) | copy-start | bytes 15364
  222.1 16.9 %copy-start.3 = (f32[4096]{0:T(1024)S(1)}, f32[4096]{0:T(1024)}, u32[]{:S(2)}) copy-start(f32[4096]{0:T(1024)} %param.32) | copy-start | bytes 49156
  226.7 11.3 %all-to-all-start = ((bf16[32,1,2,1280]{3,2,1,0:T(2,128)(2,1)}), bf16[32,1,2,1280]{3,2,1,0:T(2,128)(2,1)S(1)}, u32[]{:S(2)}, u32[]{:S(2)}) async-start(bf16[32,1,2,1280]{3,2,1,0:T(2,128)(2,1)} %broadcast_select_fusion.1), calls=%async_computation | async-start | bytes 327680 | tf_op jit(solution)/shard_map/all_to_all | solution.py:143
  230.0 49.4 %all-gather.10.cloned.1.call-start = ((), (), s32[]{:S(2)}) async-start(), calls=%async_computation.4 | async-start | bytes 5242880 | tf_op jit(solution)/shard_map/all_gather | solution.py:164
  239.0 6.3 %copy-start.4 = (f32[4096]{0:T(1024)S(1)}, f32[4096]{0:T(1024)}, u32[]{:S(2)}) copy-start(f32[4096]{0:T(1024)} %param.33) | copy-start | bytes 49156
  246.6 87.1 %all-gather.12.cloned.1.call-start = ((), (), s32[]{:S(2)}) async-start(), calls=%async_computation.5 | async-start | bytes 2359296 | tf_op jit(solution)/shard_map/all_gather | solution.py:203
  284.4 98.9 %all-gather.14.cloned.1.call-start = ((), (), s32[]{:S(2)}) async-start(), calls=%async_computation.6 | async-start | bytes 2359296 | tf_op jit(solution)/shard_map/all_gather | solution.py:204
  289.5 216.0 %reduce-scatter.2.cloned.1.call-start = ((), (), s32[]{:S(2)}) async-start(), calls=%async_computation.7 | async-start | bytes 5242880 | tf_op jit(solution)/shard_map/reduce_scatter | solution.py:240
  390.8 5.8 %copy-start.2 = (f32[2,1024,512,2]{2,1,3,0:T(8,128)S(1)}, f32[2,1024,512,2]{2,1,3,0:T(8,128)}, u32[]{:S(2)}) copy-start(f32[2,1024,512,2]{2,1,3,0:T(8,128)} %get-tuple-element.359) | copy-start | bytes 25165828 | tf_op jit(solution)/shard_map/while
  408.8 5.8 %copy-start.2 = (f32[2,1024,512,2]{2,1,3,0:T(8,128)S(1)}, f32[2,1024,512,2]{2,1,3,0:T(8,128)}, u32[]{:S(2)}) copy-start(f32[2,1024,512,2]{2,1,3,0:T(8,128)} %get-tuple-element.359) | copy-start | bytes 25165828 | tf_op jit(solution)/shard_map/while
  426.7 5.8 %copy-start.2 = (f32[2,1024,512,2]{2,1,3,0:T(8,128)S(1)}, f32[2,1024,512,2]{2,1,3,0:T(8,128)}, u32[]{:S(2)}) copy-start(f32[2,1024,512,2]{2,1,3,0:T(8,128)} %get-tuple-element.359) | copy-start | bytes 25165828 | tf_op jit(solution)/shard_map/while
  444.7 5.8 %copy-start.2 = (f32[2,1024,512,2]{2,1,3,0:T(8,128)S(1)}, f32[2,1024,512,2]{2,1,3,0:T(8,128)}, u32[]{:S(2)}) copy-start(f32[2,1024,512,2]{2,1,3,0:T(8,128)} %get-tuple-element.359) | copy-start | bytes 25165828 | tf_op jit(solution)/shard_map/while
  455.6 50.0 %copy-start.1 = (bf16[4096,256]{1,0:T(8,128)(2,1)S(1)}, bf16[4096,256]{1,0:T(8,128)(2,1)}, u32[]{:S(2)}) copy-start(bf16[4096,256]{1,0:T(8,128)(2,1)} %param.35) | copy-start | bytes 6291460
Sparse Core Ops, SparseCore 0:
  9.5 144.9 all-gather.5
  156.7 59.6 all-gather.7
  246.7 32.7 all-gather.9
  284.6 49.0 all-gather.11
  335.7 47.5 all-gather.13
  462.4 43.1 reduce-scatter.1
where the time goes:
time: 513 us; the launch traced here: 512 us
  waiting for transfers between devices  341 us (66%)
  matrix products  83.9 us (16%)
  other arithmetic  37.4 us (7%)
  local copies, waits for them, and re-layouts  24.6 us (5%)
  between operations  20.7 us (4%)
    all_gather x1, waiting for transfers between devices, per_device(): lax.all_gather(vit_qkv_w, 'seq', axis=0, tiled=True)  126 us
    all_gather x1, waiting for transfers between devices, per_device(): value_piece = lax.all_gather(values_own, 'seq', axis=0, tiled=True)  49.7 us
    all_gather x1, waiting for transfers between devices, per_device(): lax.all_gather(vit_out_w, 'seq', axis=0, tiled=True)  44.6 us
    reduce_scatter x1, waiting for transfers between devices, per_device(): lax.psum_scatter(jnp.dot(context_tok, wo, preferred_element_type=jnp.floa...  43.3 us
    all_gather x1, waiting for transfers between devices, per_device(): key_piece = lax.all_gather(keys_own, 'seq', axis=0, tiled=True)  37 us
    all_gather x1, waiting for transfers between devices, per_device(): shard_piece = lax.all_gather(normed_tok, 'frame', axis=0, tiled=True)  32 us
    dot_general x4, matrix products, visit(): jnp.einsum('qkgd,nkd->kgqn', grouped_rows, key_block, preferred_element_t...  23.4 us
    reduce_sum x4, other arithmetic, visit(): denominator = denominator * rescale + jnp.sum(expd, axis=-1)  18.6 us
  transfers between devices with their start and end apart: 8, of which 7 were waited for; matrix products, arithmetic and copies ran while one was open for 8% of the time, Pallas kernels for 0%

commit v1 on v0

--- a/solution.py
+++ b/solution.py
@@ -1,3 +1,4 @@
+import functools
 import math
 import jax
 import jax.numpy as jnp
@@ -10,6 +11,16 @@
 vit_epsilon = 1e-06
 norm_epsilon = 1e-05
 masked_score = -1e30
+
+
+def _find_sections(raw, array_dim):
+    return jnp.concatenate(
+        jax.lax.all_to_all(jnp.stack([raw] * jax.lax.axis_size("seq"), axis=0), "seq", 0, 0),
+        array_dim,
+    )
+
+
+guide_the_terms = functools.partial(_find_sections, array_dim=0)
 
 
 def partner_2(value, axis, stride):
@@ -109,7 +120,7 @@
     normed_states = (centred * lax.rsqrt(spread + vit_epsilon) * vit_ln_gain + vit_ln_bias).astype(
         jnp.bfloat16
     )
-    projected_vit = add_columns(normed_states, lax.all_gather(vit_qkv_w, "seq", axis=0, tiled=True))
+    projected_vit = add_columns(normed_states, guide_the_terms(vit_qkv_w))
     projected_vit = (projected_vit + vit_qkv_b).astype(jnp.bfloat16)
     head_size = width_vit // VHEADS
     shaped = projected_vit.reshape(slots_n, frame_max, 3, VHEADS, head_size)

time: 513 us -> 588 us (1.15)
  waiting for transfers between devices: 341 us -> 407 us
  starting transfers between devices: 4.26 us -> 11.5 us
    all_to_all x0 -> x1, waiting for transfers between devices: none -> 236 us  [_find_sections(): jax.lax.all_to_all(jnp.stack([raw] * jax.lax.axis_size('seq'), axis=0), '...]
    all_gather x1 -> x0, waiting for transfers between devices: 126 us -> none  [per_device(): lax.all_gather(vit_qkv_w, 'seq', axis=0, tiled=True)]
    all_gather x1, waiting for transfers between devices: 44.6 us -> 0.02 us  [per_device(): lax.all_gather(vit_out_w, 'seq', axis=0, tiled=True)]
    all_to_all x0 -> x1, starting transfers between devices: none -> 7.44 us  [_find_sections(): jax.lax.all_to_all(jnp.stack([raw] * jax.lax.axis_size('seq'), axis=0), '...]
  transfers between devices with their start and end apart: 8 -> 8, of which waited for: 7 -> 6; matrix products, arithmetic and copies ran while one was open for 8% -> 7% of each run, Pallas kernels for 0% -> 0%
where the time goes in v1:
time: 588 us; the launch traced here: 587 us
  waiting for transfers between devices  407 us (69%)
  matrix products  83.7 us (14%)
  other arithmetic  36.1 us (6%)
  local copies, waits for them, and re-layouts  28.4 us (5%)
  between operations  20 us (3%)
  starting transfers between devices  11.5 us (2%)
    all_to_all x1, waiting for transfers between devices, _find_sections(): jax.lax.all_to_all(jnp.stack([raw] * jax.lax.axis_size('seq'), axis=0), '...  236 us
    all_gather x1, waiting for transfers between devices, per_device(): value_piece = lax.all_gather(values_own, 'seq', axis=0, tiled=True)  49.7 us
    reduce_scatter x1, waiting for transfers between devices, per_device(): lax.psum_scatter(jnp.dot(context_tok, wo, preferred_element_type=jnp.floa...  43.3 us
    all_gather x1, waiting for transfers between devices, per_device(): key_piece = lax.all_gather(keys_own, 'seq', axis=0, tiled=True)  37 us
    all_gather x1, waiting for transfers between devices, per_device(): shard_piece = lax.all_gather(normed_tok, 'frame', axis=0, tiled=True)  32 us
    dot_general x4, matrix products, visit(): jnp.einsum('qkgd,nkd->kgqn', grouped_rows, key_block, preferred_element_t...  23.4 us
    reduce_sum x4, other arithmetic, visit(): denominator = denominator * rescale + jnp.sum(expd, axis=-1)  18.6 us
    dot_general x4, matrix products, visit(): jnp.einsum('kgqn,nkd->kgqd', expd.astype(jnp.bfloat16), value_block, pref...  18.3 us
  transfers between devices with their start and end apart: 8, of which 6 were waited for; matrix products, arithmetic and copies ran while one was open for 7% of the time, Pallas kernels for 0%

profile of v1, /device:TPU:0, one launch (start us, length us, event | category | flops | bytes accessed | tf_op | source)
XLA Modules:
  0.0 586.6 jit_solution(4126129269919485568)
XLA Ops:
  6.5 5.9 %stack.2 = bf16[8,160,3840]{2,1,0:T(8,128)(2,1)} broadcast(bf16[160,3840]{1,0:T(8,128)(2,1)} %param.27), dimensions={1,2} | broadcast | bytes 11059200 | tf_op jit(solution)/shard_map/stack | solution.py:18
  12.4 7.4 %all-to-all-start = ((bf16[8,160,3840]{2,1,0:T(8,128)(2,1)}), bf16[8,160,3840]{2,1,0:T(8,128)(2,1)}, u32[]{:S(2)}, u32[]{:S(2)}) async-start(bf16[8,160,3840]{2,1,0:T(8,128)(2,1)} %stack.2), calls=%async_computation | async-start | bytes 19660800 | tf_op jit(solution)/shard_map/all_to_all | solution.py:18
  34.9 1.9 convert_reduce_fusion
  37.1 236.3 %all-to-all-done = bf16[8,160,3840]{2,1,0:T(8,128)(2,1)} async-done(((bf16[8,160,3840]{2,1,0:T(8,128)(2,1)}), bf16[8,160,3840]{2,1,0:T(8,128)(2,1)}, u32[]{:S(2)}, u32[]{:S(2)}) %all-to-all-start) | async-done | bytes 9830432 | tf_op jit(solution)/shard_map/all_to_all | solution.py:18
  273.4 7.9 %fusion.48 = bf16[256,3840]{1,0:T(8,128)(2,1)} fusion(bf16[1280,3840]{1,0:T(8,128)(2,1)} %bitcast.7, f32[3840]{0:T(1024)S(1)} %copy-done.7, bf16[1,256,1280]{2,1,0:T(8,128)(2,1)S(1)} %get-tuple-element.277, f32[1280]{0:T(1024)S(1)} %copy-done.8, f32[1280]{0:T(1024)S(1)} %copy-done.9, f32[256]{0:T(256)S(1)} %add_rsqrt_fusion, f32[256]{0:T(256)S(1)} %broadcast_multiply_fusion), kind=kOutput, calls=%fused_computation.75 | convolution fusion | flops 2520514560 | bytes 12479488 | tf_op jit(solution)/shard_map/dot_general | solution.py:54
  281.3 4.0 copy.73
  285.3 2.0 fusion.73
  290.7 4.1 fusion.55
  301.1 3.6 all-to-all-start.1
  305.0 7.7 %all-to-all-done.1 = bf16[32,1,2,1280]{3,2,1,0:T(2,128)(2,1)S(1)} async-done(((bf16[32,1,2,1280]{3,2,1,0:T(2,128)(2,1)}), bf16[32,1,2,1280]{3,2,1,0:T(2,128)(2,1)S(1)}, u32[]{:S(2)}, u32[]{:S(2)}) %all-to-all-start.1) | async-done | bytes 163872 | tf_op jit(solution)/shard_map/all_to_all | solution.py:154
  313.7 6.1 %multiply_reduce_fusion = (f32[128]{0:T(128)S(1)}, f32[128,4096]{1,0:T(8,128)S(1)}) fusion(bf16[128,1,4096]{2,0,1:T(8,128)(2,1)} %param.24, f32[4096]{0:T(1024)S(1)} %copy-done.5, bf16[128,1280]{1,0:T(8,128)(2,1)S(1)} %gather_fusion.4, bf16[1280,4096]{1,0:T(8,128)(2,1)} %param.31, pred[128]{0:T(512)(128)(4,1)S(1)} %compare_and_fusion.1), kind=kOutput, calls=%fused_computation.93 | convolution fusion | flops 1345322880 | bytes 13976192 | tf_op jit(solution)/shard_map/dot_general | solution.py:164
  322.0 32.0 %all-gather.7.cloned.1.call-done = bf16[512,4096]{1,0:T(8,128)(2,1)} async-done(((bf16[128,4096]{1,0:T(8,128)(2,1)}), bf16[512,4096]{1,0:T(8,128)(2,1)}) %all-gather.7.cloned.1.call-update) | async-done | bytes 4194320 | tf_op jit(solution)/shard_map/all_gather | solution.py:175
  354.0 3.5 fusion.104
  359.0 4.2 convolution_convert_fusion.1
  364.2 6.0 %fusion.105 = f32[512,512]{0,1:T(8,128)S(1)} fusion(bf16[512,4096]{1,0:T(8,128)(2,1)} %all-gather.7.cloned.1.call-done, bf16[4096,512]{1,0:T(8,128)(2,1)} %param.34), kind=kOutput, calls=%fused_computation.215 | convolution fusion | flops 2147483648 | bytes 9437184 | tf_op jit(solution)/shard_map/dot_general | solution.py:178
  371.2 37.0 %all-gather.9.cloned.1.call-done = bf16[4096,2,128]{2,0,1:T(8,128)(2,1)} async-done(((bf16[512,2,128]{2,0,1:T(8,128)(2,1)}), bf16[4096,2,128]{2,0,1:T(8,128)(2,1)}) %all-gather.9.cloned.1.call-update) | async-done | bytes 2097168 | tf_op jit(solution)/shard_map/all_gather | solution.py:214
  408.2 49.7 %all-gather.11.cloned.1.call-done = bf16[4096,2,128]{2,0,1:T(8,128)(2,1)} async-done(((bf16[512,2,128]{2,0,1:T(8,128)(2,1)}), bf16[4096,2,128]{2,0,1:T(8,128)(2,1)}) %all-gather.11.cloned.1.call-update) | async-done | bytes 2097168 | tf_op jit(solution)/shard_map/all_gather | solution.py:215
  457.9 71.7 %while.20 = (s32[]{:T(128)}, f32[2,2,512]{2,1,0:T(2,128)S(1)}, f32[2,2,512]{2,1,0:T(2,128)S(1)}, f32[2,2,512,128]{3,2,1,0:T(8,128)S(1)}, s32[4]{0:T(128)S(1)}, /...) while((s32[]{:T(128)}, f32[2,2,512]{2,1,0:T(2,128)S(1)}, ...), condition=%wide.region_12.13_spmd.clone, body=%wide.region_9.12_spmd.clone.sunk | while | flops 1102377984 | bytes 64631976 | solution.py:247
  459.5 5.8 fusion.135
  465.4 4.6 fusion.137
  471.2 4.6 fusion.139
  477.5 5.8 fusion.135
  483.3 4.6 fusion.137
  489.1 4.6 fusion.139
  495.4 5.8 fusion.135
  501.3 4.6 fusion.137
  507.1 4.6 fusion.139
  513.3 5.8 fusion.135
  519.2 4.6 fusion.137
  525.0 4.6 fusion.139
  530.1 6.7 %convolution_convert_fusion = bf16[512,4096]{1,0:T(8,128)(2,1)} fusion(bf16[512,512]{0,1:T(8,128)(2,1)S(1)} %bitcast.133, bf16[512,4096]{1,0:T(8,128)(2,1)} %param.37), kind=kOutput, calls=%fused_computation.73 | convolution fusion | flops 2149580800 | bytes 8912896 | tf_op jit(solution)/shard_map/dot_general | solution.py:252
  536.8 43.3 %reduce-scatter.2.cloned.1.call-done = bf16[128,4096]{1,0:T(8,128)(2,1)} async-done(((bf16[512,4096]{1,0:T(8,128)(2,1)}), bf16[128,4096]{1,0:T(8,128)(2,1)}) %reduce-scatter.2.cloned.1.call-update) | async-done | bytes 1048592 | tf_op jit(solution)/shard_map/reduce_scatter | solution.py:251
  (133 shorter events, 36.9 us)
Async XLA Ops:
  6.5 347.5 %copy-start = (bf16[4096,256]{1,0:T(8,128)(2,1)S(1)}, bf16[4096,256]{1,0:T(8,128)(2,1)}, u32[]{:S(2)}) copy-start(bf16[4096,256]{1,0:T(8,128)(2,1)} %param.35) | copy-start | bytes 6291460
  12.4 8.2 %copy-start.11 = (s32[32]{0:T(128)S(1)}, s32[32]{0:T(128)}, u32[]{:S(2)}) copy-start(s32[32]{0:T(128)} %param.21) | copy-start | bytes 388
  12.4 11.0 %copy-start.3 = (s32[32]{0:T(128)S(1)}, s32[32]{0:T(128)}, u32[]{:S(2)}) copy-start(s32[32]{0:T(128)} %param.22) | copy-start | bytes 388
  12.4 13.6 %copy-start.2 = (s32[32]{0:T(128)S(1)}, s32[32]{0:T(128)}, u32[]{:S(2)}) copy-start(s32[32]{0:T(128)} %param.23) | copy-start | bytes 388
  12.4 261.0 %all-to-all-start = ((bf16[8,160,3840]{2,1,0:T(8,128)(2,1)}), bf16[8,160,3840]{2,1,0:T(8,128)(2,1)}, u32[]{:S(2)}, u32[]{:S(2)}) async-start(bf16[8,160,3840]{2,1,0:T(8,128)(2,1)} %stack.2), calls=%async_computation | async-start | bytes 19660800 | tf_op jit(solution)/shard_map/all_to_all | solution.py:18
  19.9 253.6 %copy-start.7 = (f32[3840]{0:T(1024)S(1)}, f32[3840]{0:T(1024)}, u32[]{:S(2)}) copy-start(f32[3840]{0:T(1024)} %param.28) | copy-start | bytes 46084
  19.9 253.6 %copy-start.8 = (f32[1280]{0:T(1024)S(1)}, f32[1280]{0:T(1024)}, u32[]{:S(2)}) copy-start(f32[1280]{0:T(1024)} %param.26) | copy-start | bytes 15364
  19.9 253.6 %copy-start.9 = (f32[1280]{0:T(1024)S(1)}, f32[1280]{0:T(1024)}, u32[]{:S(2)}) copy-start(f32[1280]{0:T(1024)} %param.25) | copy-start | bytes 15364
  19.9 270.8 %all-gather.5.cloned.1.call-start = ((), (), s32[]{:S(2)}) async-start(), calls=%async_computation.3 | async-start | bytes 3686400 | tf_op jit(solution)/shard_map/all_gather | solution.py:139
  19.9 14.9 %collective-permute-start = (bf16[2,256,1280]{2,1,0:T(8,128)(2,1)}, bf16[2,256,1280]{2,1,0:T(8,128)(2,1)}, u32[]{:S(2)}, u32[]{:S(2)}) collective-permute-start(bf16[2,256,1280]{2,1,0:T(8,128)(2,1)} %param.20), channel_id=1, source_target_pairs={{0,8},{8,0},{16,24},{24,16},{1,9},{9,1},{17,25},{25,17},{2,10},{10... | collective-permute-start | bytes 3932168 | tf_op jit(solution)/shard_map/ppermute | solution.py:29
  289.1 1.6 copy-start.10
  296.5 17.2 %copy-start.5 = (f32[4096]{0:T(1024)S(1)}, f32[4096]{0:T(1024)}, u32[]{:S(2)}) copy-start(f32[4096]{0:T(1024)} %param.32) | copy-start | bytes 49156
  301.1 11.6 %all-to-all-start.1 = ((bf16[32,1,2,1280]{3,2,1,0:T(2,128)(2,1)}), bf16[32,1,2,1280]{3,2,1,0:T(2,128)(2,1)S(1)}, u32[]{:S(2)}, u32[]{:S(2)}) async-start(bf16[32,1,2,1280]{3,2,1,0:T(2,128)(2,1)} %broadcast_select_fusion.1), calls=%async_computation.1 | async-start | bytes 327680 | tf_op jit(solution)/shard_map/all_to_all | solution.py:154
  304.7 49.3 %all-gather.7.cloned.1.call-start = ((), (), s32[]{:S(2)}) async-start(), calls=%async_computation.4 | async-start | bytes 5242880 | tf_op jit(solution)/shard_map/all_gather | solution.py:175
  313.7 6.2 %copy-start.6 = (f32[4096]{0:T(1024)S(1)}, f32[4096]{0:T(1024)}, u32[]{:S(2)}) copy-start(f32[4096]{0:T(1024)} %param.33) | copy-start | bytes 49156
  321.1 87.1 %all-gather.9.cloned.1.call-start = ((), (), s32[]{:S(2)}) async-start(), calls=%async_computation.5 | async-start | bytes 2359296 | tf_op jit(solution)/shard_map/all_gather | solution.py:214
  359.0 98.9 %all-gather.11.cloned.1.call-start = ((), (), s32[]{:S(2)}) async-start(), calls=%async_computation.6 | async-start | bytes 2359296 | tf_op jit(solution)/shard_map/all_gather | solution.py:215
  364.1 216.0 %reduce-scatter.2.cloned.1.call-start = ((), (), s32[]{:S(2)}) async-start(), calls=%async_computation.7 | async-start | bytes 5242880 | tf_op jit(solution)/shard_map/reduce_scatter | solution.py:251
  465.4 5.8 copy-start.4
  483.3 5.8 copy-start.4
  501.2 5.8 copy-start.4
  519.2 5.8 copy-start.4
  530.1 50.0 %copy-start.1 = (bf16[4096,256]{1,0:T(8,128)(2,1)S(1)}, bf16[4096,256]{1,0:T(8,128)(2,1)}, u32[]{:S(2)}) copy-start(bf16[4096,256]{1,0:T(8,128)(2,1)} %param.35) | copy-start | bytes 6291460
Sparse Core Ops, SparseCore 0:
  22.9 212.3 all-gather.4
  321.3 32.7 all-gather.6
  359.1 49.0 all-gather.8
  410.2 47.5 all-gather.10
  536.9 43.1 reduce-scatter.1
